TPU v7x, 256 devices: a whole 4x4x8 slice. The times are simulated.
256 devices in a mesh: mats: 64 (over z, x, core), tp: 4 (over y).
Axes of the slice: x: 4, y: 4, z: 8, core: 2. Of those that a mesh axis runs over, the one named last changes fastest.
Arguments:
- grad: bfloat16 [3072, 16384], P('tp', 'mats'), may hold values from -40 to 40
- momentum: float32 [3072, 16384], P('tp', 'mats'), may hold values from -6 to 6
Outputs:
- update: bfloat16 [3072, 16384], P('tp', 'mats')
- new_momentum: float32 [3072, 16384], P('tp', 'mats')
All inputs are finite; a program needn't handle non-finite values.
Results may differ from a plain program's by a relative error of at most 0.01.
Values may be sent and summed in bfloat16 or wider, within the bound.
A program may use at most 64 MiB of HBM per device.

v0:
```python
import math
import jax
import jax.numpy as jnp
from jax import lax
from jax.sharding import Mesh
from jax.sharding import PartitionSpec as P

R = 3072
C = 16384
ITERS = 2
MATS = ("mats_0", "mats_1", "mats_2")
momentum_beta = 0.95
first_coef = 3.4445
second_coef = -4.775
third_coef = 2.0315
shape_gain = 0.2
epsilon = 1e-06


def laid_out(tiles, dim):
    tiles = jnp.moveaxis(tiles, 0, dim)
    lengths = tiles.shape
    return tiles.reshape(*lengths[:dim], lengths[dim] * lengths[dim + 1], *lengths[dim + 2 :])


def sent_to_all(array, axis):
    copies = jnp.broadcast_to(array, (lax.axis_size(axis), *array.shape))
    return lax.all_to_all(copies, axis, split_axis=0, concat_axis=0, tiled=True)


def gather_directly(array, axis, dim):
    return laid_out(sent_to_all(array, axis), dim)


def gather_in_order(array, axes, sequence):
    tiles = array[None]
    for k in sequence:
        tiles = lax.all_gather(tiles, axes[k], axis=0, tiled=True)
    block = [lax.axis_size(axes[k]) for k in reversed(sequence)]
    tiles = tiles.reshape(*block, *array.shape)
    turned = sorted(range(len(sequence)), key=lambda place: sequence[len(sequence) - 1 - place])
    return tiles.transpose(*turned, *range(len(sequence), tiles.ndim)).reshape(-1, *array.shape)


def whole_of(array, axes, sequence, dim):
    return laid_out(gather_in_order(array, axes, sequence), dim)


def over_copies(array, axis):
    everything = sent_to_all(array, axis)
    return jnp.sum(everything, axis=0)


def taken_together(array, axis):
    everything = sent_to_all(array, axis)
    return jnp.max(everything, axis=0)


def row_dot(left, right):
    return lax.dot_general(
        left, right, (((1,), (1,)), ((), ())), preferred_element_type=jnp.float32
    )


def per_device(grad, momentum):
    new_momentum = momentum_beta * momentum + grad.astype(jnp.float32)
    iterate = (grad.astype(jnp.float32) + momentum_beta * new_momentum).astype(jnp.bfloat16)
    for step in range(ITERS):
        columns = gather_directly(iterate, "tp", 0)
        partial_gram = row_dot(iterate, columns)
        share = lax.psum_scatter(partial_gram, MATS, scatter_dimension=1, tiled=True).astype(
            jnp.bfloat16
        )
        gram = whole_of(share, MATS, (1, 0, 2), 1)
        if step == 0:
            share_sums = jnp.sum(jnp.abs(share.astype(jnp.float32)), axis=1)
            row_sums = over_copies(share_sums, MATS)
            bound = taken_together(jnp.max(row_sums), "tp") + epsilon
            root = lax.rsqrt(bound)
        first = jnp.dot(gram, columns, preferred_element_type=jnp.float32).astype(jnp.bfloat16)
        second = jnp.dot(
            gram, gather_directly(first, "tp", 0), preferred_element_type=jnp.float32
        ).astype(jnp.bfloat16)
        if step == 0:
            mixed = (
                first_coef * iterate.astype(jnp.float32) * root
                + second_coef * first.astype(jnp.float32) * root**3
                + third_coef * second.astype(jnp.float32) * root**5
            )
        else:
            mixed = (
                first_coef * iterate.astype(jnp.float32)
                + second_coef * first.astype(jnp.float32)
                + third_coef * second.astype(jnp.float32)
            )
        iterate = mixed.astype(jnp.bfloat16)
    update = (shape_gain * math.sqrt(max(R, C)) * iterate.astype(jnp.float32)).astype(jnp.bfloat16)
    return (update, new_momentum)


def solution(mesh):
    split = Mesh(
        mesh.devices.reshape(8, 4, 2, mesh.shape["tp"]), ("mats_0", "mats_1", "mats_2", "tp")
    )
    return jax.shard_map(
        per_device,
        mesh=split,
        in_specs=(P("tp", MATS), P("tp", MATS)),
        out_specs=(P("tp", MATS), P("tp", MATS)),
        check_vma=False,
    )
```

profile of v0, /device:TPU:1, one launch (start us, length us, event | category | flops | bytes accessed | tf_op | source)
XLA Modules:
  0.0 602.9 jit_solution(10310170198701383736)
XLA Ops:
  7.2 2.3 fusion.11
  9.6 24.7 %all_to_all.32 = bf16[4,768,256]{2,1,0:T(8,128)(2,1)S(1)} all-to-all(bf16[4,768,256]{2,1,0:T(8,128)(2,1)S(1)} %broadcast_in_dim.24), channel_id=1, replica_groups=mesh['mats_0'=8,'mats_1'=4,'mats_2'=2,'tp'=4] {'tp'}, dimensions={0} | all-to-all | bytes 3145728 | tf_op jit(solution)/shard_map/all_to_all | solution.py:28
  34.3 5.0 fusion.12
  39.4 153.2 %reduce-scatter.3.cloned.1.call-done = f32[768,48]{0,1:T(8,128)} async-done(((f32[768,3072]{0,1:T(8,128)}), f32[768,48]{0,1:T(8,128)}) %reduce-scatter.3.cloned.1.call-update) | async-done | bytes 147472 | tf_op jit(solution)/shard_map/reduce_scatter | solution.py:71
  192.6 0.9 abs_reduce_fusion
  193.5 9.4 %all-gather = bf16[3072,48]{0,1:T(8,128)(2,1)S(1)} all-gather(bf16[768,48]{0,1:T(8,128)(2,1)S(1)} %get-tuple-element.3), channel_id=2, replica_groups=mesh['mats_0'=8,'mats_1'=4,'mats_2'=2,'tp'=4] {'mats_1'}, dimensions={0}, use_global_device_ids=true | all-gather | bytes 368640 | tf_op jit(solution)/shard_map/all_gather | solution.py:38
  202.9 0.7 copy.30
  203.8 43.3 %all-gather.7.cloned.1.call-done = bf16[32,768,48]{1,2,0:T(8,128)(2,1)} async-done(((bf16[4,768,48]{1,2,0:T(8,128)(2,1)}), bf16[32,768,48]{1,2,0:T(8,128)(2,1)}) %all-gather.7.cloned.1.call-update) | async-done | bytes 2359312 | tf_op jit(solution)/shard_map/all_gather | solution.py:38
  247.2 23.6 %all_to_all.33 = f32[64,1,768]{2,1,0:T(1,128)S(1)} all-to-all(f32[64,1,768]{2,1,0:T(1,128)S(1)} %broadcast_in_dim.25), channel_id=1, replica_groups=mesh['mats_0'=8,'mats_1'=4,'mats_2'=2,'tp'=4] {'mats_0','mats_1','mats_2'}, dimensions={0} | all-to-all | bytes 393216 | tf_op jit(solution)/shard_map/all_to_all | solution.py:28
  270.9 0.6 reduce_max.18
  271.5 1.1 broadcast_in_dim.26
  272.6 4.0 all-to-all-start.2
  276.6 2.9 copy.19
  279.5 2.1 copy-done
  281.7 1.4 convolution_convert_fusion.3
  283.1 1.3 broadcast_in_dim.28
  284.4 4.2 all-to-all-start.3
  288.6 0.6 reduce_max.19
  289.9 18.3 %all-to-all-done.3 = bf16[4,768,256]{2,1,0:T(8,128)(2,1)S(1)} async-done(((bf16[4,768,256]{2,1,0:T(8,128)(2,1)}), bf16[4,768,256]{2,1,0:T(8,128)(2,1)S(1)}, u32[]{:S(2)}, u32[]{:S(2)}) %all-to-all-start.3) | async-done | bytes 1572896 | tf_op jit(solution)/shard_map/all_to_all | solution.py:28
  308.2 3.8 fusion.9
  312.1 20.9 %all_to_all.34 = bf16[4,768,256]{2,1,0:T(8,128)(2,1)S(1)} all-to-all(bf16[4,768,256]{2,1,0:T(8,128)(2,1)S(1)} %broadcast_in_dim.29), channel_id=1, replica_groups=mesh['mats_0'=8,'mats_1'=4,'mats_2'=2,'tp'=4] {'tp'}, dimensions={0} | all-to-all | bytes 3145728 | tf_op jit(solution)/shard_map/all_to_all | solution.py:28
  332.9 5.0 fusion.13
  338.1 148.1 %reduce-scatter.5.cloned.1.call-done = f32[768,48]{0,1:T(8,128)} async-done(((f32[768,3072]{0,1:T(8,128)}), f32[768,48]{0,1:T(8,128)}) %reduce-scatter.5.cloned.1.call-update) | async-done | bytes 147472 | tf_op jit(solution)/shard_map/reduce_scatter | solution.py:71
  486.1 0.9 convert_element_type.69
  487.1 9.4 %all-gather.1 = bf16[3072,48]{0,1:T(8,128)(2,1)S(1)} all-gather(bf16[768,48]{0,1:T(8,128)(2,1)S(1)} %convert_element_type.69), channel_id=3, replica_groups=mesh['mats_0'=8,'mats_1'=4,'mats_2'=2,'tp'=4] {'mats_1'}, dimensions={0}, use_global_device_ids=true | all-gather | bytes 368640 | tf_op jit(solution)/shard_map/all_gather | solution.py:38
  496.5 0.7 copy.29
  497.3 43.7 %all-gather.11.cloned.1.call-done = bf16[32,768,48]{1,2,0:T(8,128)(2,1)} async-done(((bf16[4,768,48]{1,2,0:T(8,128)(2,1)}), bf16[32,768,48]{1,2,0:T(8,128)(2,1)}) %all-gather.11.cloned.1.call-update) | async-done | bytes 2359312 | tf_op jit(solution)/shard_map/all_gather | solution.py:38
  541.0 24.6 %all-gather.13.cloned.1.call-done = bf16[64,768,48]{1,2,0:T(8,128)(2,1)} async-done(((bf16[32,768,48]{1,2,0:T(8,128)(2,1)}), bf16[64,768,48]{1,2,0:T(8,128)(2,1)}) %all-gather.13.cloned.1.call-update) | async-done | bytes 4718608 | tf_op jit(solution)/shard_map/all_gather | solution.py:38
  565.6 2.9 copy.21
  568.5 1.4 convolution_convert_fusion.1
  570.0 23.9 %all_to_all.35 = bf16[4,768,256]{2,1,0:T(8,128)(2,1)S(1)} all-to-all(bf16[4,768,256]{2,1,0:T(8,128)(2,1)S(1)} %broadcast_in_dim.31), channel_id=1, replica_groups=mesh['mats_0'=8,'mats_1'=4,'mats_2'=2,'tp'=4] {'tp'}, dimensions={0} | all-to-all | bytes 3145728 | tf_op jit(solution)/shard_map/all_to_all | solution.py:28
  593.9 2.2 fusion.10
  (20 shorter events, 0.9 us)
Async XLA Ops:
  7.2 185.4 %reduce-scatter.3.cloned.1.call-start = ((), (), s32[]{:S(2)}) async-start(), calls=%async_computation.8 | async-start | bytes 9584640 | tf_op jit(solution)/shard_map/reduce_scatter | solution.py:71
  39.3 207.7 %all-gather.7.cloned.1.call-start = ((), (), s32[]{:S(2)}) async-start(), calls=%async_computation.9 | async-start | bytes 2654208 | tf_op jit(solution)/shard_map/all_gather | solution.py:38
  203.7 72.9 %all-gather.9.cloned.1.call-start = ((), (), s32[]{:S(2)}) async-start(), calls=%async_computation.10 | async-start | bytes 7077888 | tf_op jit(solution)/shard_map/all_gather | solution.py:38
  272.6 10.5 %all-to-all-start.2 = ((f32[4,1,1]{2,1,0:T(1,128)}), f32[4,1,1]{2,1,0:T(1,128)S(1)}, u32[]{:S(2)}, u32[]{:S(2)}) async-start(f32[4,1,1]{2,1,0:T(1,128)} %broadcast_in_dim.26), calls=%async_computation.3 | async-start | bytes 4096 | tf_op jit(solution)/shard_map/all_to_all | solution.py:28
  279.5 2.1 copy-start
  284.4 23.8 %all-to-all-start.3 = ((bf16[4,768,256]{2,1,0:T(8,128)(2,1)}), bf16[4,768,256]{2,1,0:T(8,128)(2,1)S(1)}, u32[]{:S(2)}, u32[]{:S(2)}) async-start(bf16[4,768,256]{2,1,0:T(8,128)(2,1)} %broadcast_in_dim.28), calls=%async_computation.4 | async-start | bytes 3145728 | tf_op jit(solution)/shard_map/all_to_all | solution.py:28
  288.6 197.5 %reduce-scatter.5.cloned.1.call-start = ((), (), s32[]{:S(2)}) async-start(), calls=%async_computation.11 | async-start | bytes 9584640 | tf_op jit(solution)/shard_map/reduce_scatter | solution.py:71
  338.0 203.0 %all-gather.11.cloned.1.call-start = ((), (), s32[]{:S(2)}) async-start(), calls=%async_computation.12 | async-start | bytes 2654208 | tf_op jit(solution)/shard_map/all_gather | solution.py:38
  497.3 68.3 %all-gather.13.cloned.1.call-start = ((), (), s32[]{:S(2)}) async-start(), calls=%async_computation.13 | async-start | bytes 7077888 | tf_op jit(solution)/shard_map/all_gather | solution.py:38
Sparse Core Ops, SparseCore 0:
  39.4 153.0 reduce-scatter.2
  203.8 43.1 all-gather.6
  248.9 22.8 all-gather.8
  338.1 147.9 reduce-scatter.4
  497.4 43.5 all-gather.10
  542.6 22.8 all-gather.12
where the time goes:
time: 603 us
  waiting for transfers between devices  431 us (71%)
  blocking collectives  112 us (19%)
  matrix products  18.9 us (3%)
  between operations  14.9 us (2%)
  local copies, waits for them, and re-layouts  12.2 us (2%)
  starting transfers between devices  8.45 us (1%)
    reduce_scatter x2, waiting for transfers between devices, per_device(): lax.psum_scatter(partial_gram, MATS, scatter_dimension=1, tiled=True)  301 us
    all_gather x4, waiting for transfers between devices, gather_in_order(): tiles = lax.all_gather(tiles, axes[k], axis=0, tiled=True)  112 us
    all_to_all x4, blocking collectives, sent_to_all(): return lax.all_to_all(copies, axis, split_axis=0, concat_axis=0, tiled=True)  93 us
    all_gather x2, blocking collectives, gather_in_order(): tiles = lax.all_gather(tiles, axes[k], axis=0, tiled=True)  18.9 us
    all_to_all x2, waiting for transfers between devices, sent_to_all(): return lax.all_to_all(copies, axis, split_axis=0, concat_axis=0, tiled=True)  18.3 us
  transfers between devices with their start and end apart: 8, of which 6 were waited for; matrix products, arithmetic and copies ran while one was open for 1% of the time, Pallas kernels for 0%

commit v1 on v0

--- a/solution.py
+++ b/solution.py
@@ -35,7 +35,9 @@
 def gather_in_order(array, axes, sequence):
     tiles = array[None]
     for k in sequence:
-        tiles = lax.all_gather(tiles, axes[k], axis=0, tiled=True)
+        tiles = jnp.concatenate(
+            lax.all_to_all(jnp.stack([tiles] * lax.axis_size(axes[k])), axes[k], 0, 0), axis=0
+        )
     block = [lax.axis_size(axes[k]) for k in reversed(sequence)]
     tiles = tiles.reshape(*block, *array.shape)
     turned = sorted(range(len(sequence)), key=lambda place: sequence[len(sequence) - 1 - place])

time: 603 us -> 629 us (1.043)
  blocking collectives: 112 us -> 189 us
  waiting for transfers between devices: 431 us -> 375 us
    all_gather x4 -> x0, waiting for transfers between devices: 112 us -> none  [gather_in_order(): tiles = lax.all_gather(tiles, axes[k], axis=0, tiled=True)]
    all_to_all x0 -> x5, blocking collectives: none -> 95 us  [gather_in_order(): lax.all_to_all(jnp.stack([tiles] * lax.axis_size(axes[k])), axes[k], 0, 0)]
    all_to_all x0 -> x1, waiting for transfers between devices: none -> 56.7 us  [gather_in_order(): lax.all_to_all(jnp.stack([tiles] * lax.axis_size(axes[k])), axes[k], 0, 0)]
    all_gather x2 -> x0, blocking collectives: 18.9 us -> none  [gather_in_order(): tiles = lax.all_gather(tiles, axes[k], axis=0, tiled=True)]
  transfers between devices with their start and end apart: 8 -> 5, of which waited for: 6 -> 4; matrix products, arithmetic and copies ran while one was open for 1% -> 1% of each run, Pallas kernels for 0% -> 0%
where the time goes in v1:
time: 629 us
  waiting for transfers between devices  375 us (60%)
  blocking collectives  189 us (30%)
  matrix products  18.9 us (3%)
  between operations  14.9 us (2%)
  starting transfers between devices  12.6 us (2%)
  local copies, waits for them, and re-layouts  10.2 us (2%)
  other arithmetic  8.68 us (1%)
    reduce_scatter x2, waiting for transfers between devices, per_device(): lax.psum_scatter(partial_gram, MATS, scatter_dimension=1, tiled=True)  300 us
    all_to_all x5, blocking collectives, gather_in_order(): lax.all_to_all(jnp.stack([tiles] * lax.axis_size(axes[k])), axes[k], 0, 0)  95 us
    all_to_all x4, blocking collectives, sent_to_all(): return lax.all_to_all(copies, axis, split_axis=0, concat_axis=0, tiled=True)  93.6 us
    all_to_all x1, waiting for transfers between devices, gather_in_order(): lax.all_to_all(jnp.stack([tiles] * lax.axis_size(axes[k])), axes[k], 0, 0)  56.7 us
    all_to_all x2, waiting for transfers between devices, sent_to_all(): return lax.all_to_all(copies, axis, split_axis=0, concat_axis=0, tiled=True)  18.3 us
  transfers between devices with their start and end apart: 5, of which 4 were waited for; matrix products, arithmetic and copies ran while one was open for 1% of the time, Pallas kernels for 0%

profile of v1, /device:TPU:1, one launch (start us, length us, event | category | flops | bytes accessed | tf_op | source)
XLA Modules:
  0.0 628.6 jit_solution(12237874487786093101)
XLA Ops:
  7.2 2.3 fusion.11
  9.6 24.7 %all_to_all.62 = bf16[4,768,256]{2,1,0:T(8,128)(2,1)S(1)} all-to-all(bf16[4,768,256]{2,1,0:T(8,128)(2,1)S(1)} %broadcast_in_dim.18), channel_id=1, replica_groups=mesh['mats_0'=8,'mats_1'=4,'mats_2'=2,'tp'=4] {'tp'}, dimensions={0} | all-to-all | bytes 3145728 | tf_op jit(solution)/shard_map/all_to_all | solution.py:28
  34.3 5.0 fusion.12
  39.3 153.6 %reduce-scatter.3.cloned.1.call-done = f32[768,48]{0,1:T(8,128)} async-done(((f32[768,3072]{0,1:T(8,128)}), f32[768,48]{0,1:T(8,128)}) %reduce-scatter.3.cloned.1.call-update) | async-done | bytes 147472 | tf_op jit(solution)/shard_map/reduce_scatter | solution.py:73
  192.9 0.9 abs_reduce_fusion
  193.8 8.5 %all_to_all.63 = bf16[4,1,768,48]{2,3,1,0:T(8,128)(2,1)S(1)} all-to-all(bf16[4,1,768,48]{2,3,1,0:T(8,128)(2,1)S(1)} %stack.18), channel_id=1, replica_groups=mesh['mats_0'=8,'mats_1'=4,'mats_2'=2,'tp'=4] {'mats_1'}, dimensions={0} | all-to-all | bytes 589824 | tf_op jit(solution)/shard_map/all_to_all | solution.py:39
  202.5 24.3 %all_to_all.64 = f32[64,1,768]{2,1,0:T(1,128)S(1)} all-to-all(f32[64,1,768]{2,1,0:T(1,128)S(1)} %broadcast_in_dim.19), channel_id=1, replica_groups=mesh['mats_0'=8,'mats_1'=4,'mats_2'=2,'tp'=4] {'mats_0','mats_1','mats_2'}, dimensions={0} | all-to-all | bytes 393216 | tf_op jit(solution)/shard_map/all_to_all | solution.py:28
  226.8 1.6 stack.19
  228.4 4.4 all-to-all-start.4
  233.5 56.7 %all-to-all-done.4 = bf16[8,4,768,48]{2,3,1,0:T(8,128)(2,1)} async-done(((bf16[8,4,768,48]{2,3,1,0:T(8,128)(2,1)}), bf16[8,4,768,48]{2,3,1,0:T(8,128)(2,1)}, u32[]{:S(2)}, u32[]{:S(2)}) %all-to-all-start.4) | async-done | bytes 2359328 | tf_op jit(solution)/shard_map/all_to_all | solution.py:39
  290.2 2.8 pad_maximum_fusion
  293.0 8.7 %all_to_all.65 = bf16[2,32,768,48]{2,3,1,0:T(8,128)(2,1)} all-to-all(bf16[2,32,768,48]{2,3,1,0:T(8,128)(2,1)S(1)} %pad_maximum_fusion), channel_id=1, replica_groups=mesh['mats_0'=8,'mats_1'=4,'mats_2'=2,'tp'=4] {'mats_2'}, dimensions={0} | all-to-all | bytes 9437184 | tf_op jit(solution)/shard_map/all_to_all | solution.py:39
  301.7 1.1 broadcast_in_dim.20
  302.8 4.0 all-to-all-start.2
  306.8 2.9 copy.12
  309.7 2.1 copy-done
  311.8 1.4 convolution_convert_fusion.3
  313.2 1.3 broadcast_in_dim.21
  314.5 4.2 all-to-all-start.6
  320.1 18.3 %all-to-all-done.6 = bf16[4,768,256]{2,1,0:T(8,128)(2,1)S(1)} async-done(((bf16[4,768,256]{2,1,0:T(8,128)(2,1)}), bf16[4,768,256]{2,1,0:T(8,128)(2,1)S(1)}, u32[]{:S(2)}, u32[]{:S(2)}) %all-to-all-start.6) | async-done | bytes 1572896 | tf_op jit(solution)/shard_map/all_to_all | solution.py:28
  338.4 3.8 fusion.9
  342.2 20.9 %all_to_all.66 = bf16[4,768,256]{2,1,0:T(8,128)(2,1)S(1)} all-to-all(bf16[4,768,256]{2,1,0:T(8,128)(2,1)S(1)} %broadcast_in_dim.22), channel_id=1, replica_groups=mesh['mats_0'=8,'mats_1'=4,'mats_2'=2,'tp'=4] {'tp'}, dimensions={0} | all-to-all | bytes 3145728 | tf_op jit(solution)/shard_map/all_to_all | solution.py:28
  363.1 5.0 fusion.13
  368.2 146.2 %reduce-scatter.5.cloned.1.call-done = f32[768,48]{0,1:T(8,128)} async-done(((f32[768,3072]{0,1:T(8,128)}), f32[768,48]{0,1:T(8,128)}) %reduce-scatter.5.cloned.1.call-update) | async-done | bytes 147472 | tf_op jit(solution)/shard_map/reduce_scatter | solution.py:73
  514.4 0.9 convert_element_type.69
  515.4 9.0 %all_to_all.67 = bf16[4,1,768,48]{2,3,1,0:T(8,128)(2,1)S(1)} all-to-all(bf16[4,1,768,48]{2,3,1,0:T(8,128)(2,1)S(1)} %stack.21), channel_id=1, replica_groups=mesh['mats_0'=8,'mats_1'=4,'mats_2'=2,'tp'=4] {'mats_1'}, dimensions={0} | all-to-all | bytes 589824 | tf_op jit(solution)/shard_map/all_to_all | solution.py:39
  524.5 52.7 %all_to_all.68 = bf16[8,4,768,48]{2,3,1,0:T(8,128)(2,1)S(1)} all-to-all(bf16[8,4,768,48]{2,3,1,0:T(8,128)(2,1)S(1)} %stack.22), channel_id=1, replica_groups=mesh['mats_0'=8,'mats_1'=4,'mats_2'=2,'tp'=4] {'mats_0'}, dimensions={0} | all-to-all | bytes 4718592 | tf_op jit(solution)/shard_map/all_to_all | solution.py:39
  577.6 16.1 %all_to_all.69 = bf16[2,32,768,48]{2,3,1,0:T(8,128)(2,1)S(1)} all-to-all(bf16[2,32,768,48]{2,3,1,0:T(8,128)(2,1)S(1)} %pad_maximum_fusion.1), channel_id=1, replica_groups=mesh['mats_0'=8,'mats_1'=4,'mats_2'=2,'tp'=4] {'mats_2'}, dimensions={0} | all-to-all | bytes 9437184 | tf_op jit(solution)/shard_map/all_to_all | solution.py:39
  593.7 0.6 copy.13
  594.3 1.4 convolution_convert_fusion.1
  595.9 23.7 %all_to_all.70 = bf16[4,768,256]{2,1,0:T(8,128)(2,1)S(1)} all-to-all(bf16[4,768,256]{2,1,0:T(8,128)(2,1)S(1)} %broadcast_in_dim.23), channel_id=1, replica_groups=mesh['mats_0'=8,'mats_1'=4,'mats_2'=2,'tp'=4] {'tp'}, dimensions={0} | all-to-all | bytes 3145728 | tf_op jit(solution)/shard_map/all_to_all | solution.py:28
  619.6 2.2 fusion.10
  (17 shorter events, 2.5 us)
Async XLA Ops:
  7.2 185.7 %reduce-scatter.3.cloned.1.call-start = ((), (), s32[]{:S(2)}) async-start(), calls=%async_computation.14 | async-start | bytes 9584640 | tf_op jit(solution)/shard_map/reduce_scatter | solution.py:73
  228.4 61.8 %all-to-all-start.4 = ((bf16[8,4,768,48]{2,3,1,0:T(8,128)(2,1)}), bf16[8,4,768,48]{2,3,1,0:T(8,128)(2,1)}, u32[]{:S(2)}, u32[]{:S(2)}) async-start(bf16[8,4,768,48]{2,3,1,0:T(8,128)(2,1)} %stack.19), calls=%async_computation.5 | async-start | bytes 4718592 | tf_op jit(solution)/shard_map/all_to_all | solution.py:39
  302.8 10.4 %all-to-all-start.2 = ((f32[4,1,1]{2,1,0:T(1,128)}), f32[4,1,1]{2,1,0:T(1,128)S(1)}, u32[]{:S(2)}, u32[]{:S(2)}) async-start(f32[4,1,1]{2,1,0:T(1,128)} %broadcast_in_dim.20), calls=%async_computation.3 | async-start | bytes 4096 | tf_op jit(solution)/shard_map/all_to_all | solution.py:28
  309.7 2.1 copy-start
  314.5 23.8 %all-to-all-start.6 = ((bf16[4,768,256]{2,1,0:T(8,128)(2,1)}), bf16[4,768,256]{2,1,0:T(8,128)(2,1)S(1)}, u32[]{:S(2)}, u32[]{:S(2)}) async-start(bf16[4,768,256]{2,1,0:T(8,128)(2,1)} %broadcast_in_dim.21), calls=%async_computation.7 | async-start | bytes 3145728 | tf_op jit(solution)/shard_map/all_to_all | solution.py:28
  318.8 195.6 %reduce-scatter.5.cloned.1.call-start = ((), (), s32[]{:S(2)}) async-start(), calls=%async_computation.15 | async-start | bytes 9584640 | tf_op jit(solution)/shard_map/reduce_scatter | solution.py:73
Sparse Core Ops, SparseCore 0:
  39.4 153.3 reduce-scatter.2
  368.3 146.0 reduce-scatter.4
